TPU v7x, 32 devices: a whole 2x2x4 slice. The times are simulated.
32 devices in a mesh: seq: 8 (over y, x, core), head: 4 (over z).
Axes of the slice: x: 2, y: 2, z: 4, core: 2. Of those that a mesh axis runs over, the one named last changes fastest.
Arguments:
- queries: bfloat16 [1024, 1024], P('seq', 'head'), may hold values from -24 to 24
- keys_values: bfloat16 [2, 1024, 128], P(None, 'seq'), may hold values from -6 to 6
- out_weight: bfloat16 [2560, 8, 128], P('head'), may hold values from -0.125 to 0.125
- out_grad: bfloat16 [1024, 2560], P('seq'), may hold values from -6 to 6
- positions: int32 [1024], replicated, may hold values from 0 to 1023, as said below
Outputs:
- d_query: bfloat16 [1024, 1024], P('seq', 'head')
- d_out_weight: float32 [2560, 8, 128], P('seq', 'head')
Inputs may be any that keep to these rules, and one draw needn't show every extreme that they name: positions holds each of 0 to 1023 once, in runs of 64 consecutive rows with consecutive positions, each run starting at a row and a position that are multiples of 64.
All inputs are finite; a program needn't handle non-finite values.
Results may differ from a plain program's by a relative error of at most 0.007.
Values may be sent and summed in bfloat16 or wider, within the bound.
No kernel may reach another device: no remote copies, remote signals or barrier semaphores. Data moves between devices by JAX's collectives and lax.ppermute only.
A program may use at most 64 MiB of HBM per device.

v0:
```python
import math
import jax
import jax.numpy as jnp
from jax import lax
from jax.sharding import PartitionSpec as P

HD = 128
GROUP = 8
big_negative = -1e30


def attend_block(query_rows, query_pos, block_kv, key_pos, scale):
    scores = (
        lax.dot_general(
            query_rows, block_kv[0], (((1,), (1,)), ((), ())), preferred_element_type=jnp.float32
        )
        * scale
    )
    visible = key_pos[None, :] <= query_pos[:, None]
    return (jnp.where(visible, scores, big_negative), visible)


def sweep(step_fn, states, key_piece, offset, positions):
    span_size = key_piece.shape[1]
    block_size = math.gcd(span_size, 1024)

    def step(step_index, inner):
        block_kv = lax.dynamic_slice_in_dim(key_piece, step_index * block_size, block_size, 1)
        key_pos = lax.dynamic_slice_in_dim(
            positions, offset + step_index * block_size, block_size, 0
        )
        return step_fn(inner, block_kv, key_pos)

    return lax.fori_loop(0, span_size // block_size, step, states)


def body(queries, keys_values, out_weight, out_grad, positions):
    token_count = queries.shape[0]
    head_count = queries.shape[1] // HD
    scale = HD ** (-0.5)
    seq_index = lax.axis_index("seq")
    head_index = lax.axis_index("head")
    kv_group = head_index * head_count // GROUP
    own_kv = lax.dynamic_slice_in_dim(keys_values, kv_group * HD, HD, 2)
    own_pos = lax.dynamic_slice_in_dim(positions, seq_index * token_count, token_count, 0)
    query_pos = jnp.repeat(own_pos, head_count)
    query_rows = queries.reshape(token_count * head_count, HD)
    d_attn = jnp.einsum(
        "td,dhc->thc",
        out_grad,
        lax.all_to_all(out_weight, "head", split_axis=1, concat_axis=0, tiled=True),
        preferred_element_type=jnp.float32,
    )
    d_attn = d_attn.astype(jnp.bfloat16).reshape(token_count * head_count, HD)
    row_total = token_count * head_count
    zeros_col = jnp.zeros((row_total, 1), jnp.float32)
    zeros_rows = jnp.zeros((row_total, HD), jnp.float32)
    lowest_col = jnp.full((row_total, 1), big_negative, jnp.float32)
    all_kv = lax.all_gather(own_kv, "seq", axis=1, tiled=True)

    def run_sweep(step_fn, init):
        return sweep(step_fn, init, all_kv, 0, positions)

    def stats_step(states, block_kv, key_pos):
        top, norm = states
        scores, visible = attend_block(query_rows, query_pos, block_kv, key_pos, scale)
        new_top = jnp.maximum(top, jnp.max(scores, axis=1, keepdims=True))
        weights = jnp.where(visible, jnp.exp(scores - new_top), 0.0)
        norm = jnp.exp(top - new_top) * norm + jnp.sum(weights, axis=1, keepdims=True)
        return (new_top, norm)

    top, norm = run_sweep(stats_step, (lowest_col, zeros_col))

    def block_probs(block_kv, key_pos):
        scores, visible = attend_block(query_rows, query_pos, block_kv, key_pos, scale)
        return jnp.where(visible, jnp.exp(scores - top), 0.0) / norm

    def out_step(acc_out, block_kv, key_pos):
        probs = block_probs(block_kv, key_pos)
        return acc_out + jnp.dot(
            probs.astype(jnp.bfloat16), block_kv[1], preferred_element_type=jnp.float32
        )

    attn_full = run_sweep(out_step, zeros_rows)
    delta = jnp.sum(d_attn.astype(jnp.float32) * attn_full, axis=1, keepdims=True)

    def grad_step(acc_grad, block_kv, key_pos):
        probs = block_probs(block_kv, key_pos)
        dprob = lax.dot_general(
            d_attn, block_kv[1], (((1,), (1,)), ((), ())), preferred_element_type=jnp.float32
        )
        dscore = (probs * (dprob - delta)).astype(jnp.bfloat16)
        return acc_grad + jnp.dot(dscore, block_kv[0], preferred_element_type=jnp.float32)

    d_rows = run_sweep(grad_step, zeros_rows) * scale
    attn = attn_full.astype(jnp.bfloat16).reshape(token_count, head_count, HD)
    d_query = d_rows.astype(jnp.bfloat16).reshape(token_count, head_count * HD)
    d_out_weight = lax.psum_scatter(
        jnp.einsum("td,thc->dhc", out_grad, attn, preferred_element_type=jnp.float32),
        "seq",
        scatter_dimension=0,
        tiled=True,
    )
    return (d_query, d_out_weight)


def solution(mesh):
    return jax.shard_map(
        body,
        mesh=mesh,
        in_specs=(
            P("seq", "head"),
            P(None, "seq", None),
            P("head", None, None),
            P("seq", None),
            P(),
        ),
        out_specs=(P("seq", "head"), P("seq", "head", None)),
        check_vma=False,
    )
```

profile of v0, /device:TPU:0, one launch (start us, length us, event | category | flops | bytes accessed | tf_op | source)
XLA Modules:
  0.0 125.0 jit_solution(11164809730574350599)
XLA Ops:
  7.2 0.0 copy-start
  7.2 2.6 %copy.14 = bf16[640,8,128]{2,0,1:T(8,128)(2,1)} copy(bf16[640,8,128]{2,1,0:T(8,128)(2,1)} %param.7) | data formatting | bytes 2621440 | tf_op args[2]
  9.8 0.0 copy-start.8
  9.8 0.0 copy-start.9
  9.8 0.0 copy-start.7
  9.8 6.5 %all-to-all-start = ((bf16[640,8,128]{2,0,1:T(8,128)(2,1)}), bf16[640,8,128]{2,0,1:T(8,128)(2,1)S(1)}, u32[]{:S(2)}, u32[]{:S(2)}) async-start(bf16[640,8,128]{2,0,1:T(8,128)(2,1)} %copy.14), calls=%async_computation | async-start | bytes 2621440 | tf_op jit(solution)/shard_map/all_to_all | solution.py:51
  16.3 0.0 all-reduce.3.cloned.1.call-start
  16.3 0.0 copy-done.8
  16.3 0.0 copy-done.9
  16.3 0.1 dynamic_slice.16
  16.4 0.1 broadcast_in_dim.38
  16.5 0.1 le.51
  16.7 0.0 copy-done.7
  16.7 9.9 %all_gather.3 = bf16[2,1024,128]{2,1,0:T(8,128)(2,1)S(1)} all-gather(bf16[2,128,128]{2,1,0:T(8,128)(2,1)S(1)} %copy-done.7), channel_id=1, replica_groups=mesh['seq'=8,'head'=4] {'seq'}, dimensions={1}, use_global_device_ids=true | all-gather | bytes 589824 | tf_op jit(solution)/shard_map/all_gather | solution.py:59
  26.5 0.0 copy-start.3
  26.5 0.4 fusion.15
  26.9 0.4 fusion.7
  27.3 0.3 fusion.6
  27.6 0.0 copy-start.1
  27.6 20.0 %all-to-all-done = bf16[640,8,128]{2,0,1:T(8,128)(2,1)S(1)} async-done(((bf16[640,8,128]{2,0,1:T(8,128)(2,1)}), bf16[640,8,128]{2,0,1:T(8,128)(2,1)S(1)}, u32[]{:S(2)}, u32[]{:S(2)}) %all-to-all-start) | async-done | bytes 1310752 | tf_op jit(solution)/shard_map/all_to_all | solution.py:51
  47.6 0.1 copy.15
  47.7 0.0 copy-done
  47.7 0.4 convolution_convert_fusion
  48.1 0.1 copy.16
  48.2 0.0 copy-start.5
  48.2 0.0 copy-done.3
  48.2 0.0 copy-done.1
  48.2 0.4 fusion.14
  48.6 0.2 copy-done.5
  48.8 0.5 convolution_bitcast_fusion
  49.3 3.1 %copy.18 = f32[2560,2,128]{2,1,0:T(2,128)} copy(f32[2560,2,128]{0,2,1:T(8,128)S(1)} %convolution_bitcast_fusion) | data formatting | bytes 5242880 | tf_op jit(solution)/shard_map/td,thc->dhc/dot_general | solution.py:99
  52.5 0.0 copy-start.10
  52.5 0.0 copy-start.2
  52.5 0.0 copy-start.4
  52.5 0.0 copy-start.6
  52.5 0.0 all-reduce.3.cloned.1.call-update
  52.5 0.6 copy-done.10
  53.1 0.6 dynamic-slice
  54.4 0.0 copy-done.2
  54.4 0.0 copy-done.4
  54.4 0.0 copy-done.6
  54.4 0.4 fusion.5
  54.8 0.7 reshape.37
  55.5 60.9 %all-reduce.3.cloned.1.call-done = f32[2560,2,128]{2,1,0:T(2,128)} async-done(((f32[2560,2,128]{2,1,0:T(2,128)}), f32[2560,2,128]{2,1,0:T(2,128)}) %all-reduce.3.cloned.1.call-update) | async-done | bytes 2621456
  116.4 1.7 %constant_dynamic-slice_fusion = f32[320,2,128]{2,1,0:T(2,128)} fusion(f32[2560,2,128]{2,1,0:T(2,128)} %all-reduce.3.cloned.1.call-done, u32[]{:T(128)S(6)} %multiply.1), kind=kLoop, calls=%fused_computation.23 | loop fusion | bytes 655364
  (3 shorter events, 0.0 us)
Async XLA Ops:
  7.2 40.6 %copy-start = (bf16[128,2560]{1,0:T(8,128)(2,1)S(1)}, bf16[128,2560]{1,0:T(8,128)(2,1)}, u32[]{:S(2)}) copy-start(bf16[128,2560]{1,0:T(8,128)(2,1)} %param.8) | copy-start | bytes 1966084
  9.8 6.5 %copy-start.8 = (bf16[128,256]{1,0:T(8,128)(2,1)S(1)}, bf16[128,256]{1,0:T(8,128)(2,1)}, u32[]{:S(2)}) copy-start(bf16[128,256]{1,0:T(8,128)(2,1)} %param.5) | copy-start | bytes 196612
  9.8 6.5 %copy-start.9 = (s32[1024]{0:T(1024)S(1)}, s32[1024]{0:T(1024)}, u32[]{:S(2)}) copy-start(s32[1024]{0:T(1024)} %param.9) | copy-start | bytes 12292
  9.8 6.8 %copy-start.7 = (bf16[2,128,128]{2,1,0:T(8,128)(2,1)S(1)}, bf16[2,128,128]{2,1,0:T(8,128)(2,1)}, u32[]{:S(2)}) copy-start(bf16[2,128,128]{2,1,0:T(8,128)(2,1)} %param.6) | copy-start | bytes 196612
  9.8 37.8 %all-to-all-start = ((bf16[640,8,128]{2,0,1:T(8,128)(2,1)}), bf16[640,8,128]{2,0,1:T(8,128)(2,1)S(1)}, u32[]{:S(2)}, u32[]{:S(2)}) async-start(bf16[640,8,128]{2,0,1:T(8,128)(2,1)} %copy.14), calls=%async_computation | async-start | bytes 2621440 | tf_op jit(solution)/shard_map/all_to_all | solution.py:51
  16.3 100.1 %all-reduce.3.cloned.1.call-start = ((), (), s32[]{:S(2)}) async-start(), calls=%async_computation.1 | async-start | bytes 5242880
  26.5 21.7 %copy-start.3 = (bf16[2,1024,128]{2,1,0:T(8,128)(2,1)}, bf16[2,1024,128]{2,1,0:T(8,128)(2,1)S(1)}, u32[]{:S(2)}) copy-start(bf16[2,1024,128]{2,1,0:T(8,128)(2,1)S(1)} %all_gather.3) | copy-start | bytes 1572868
  27.6 20.6 %copy-start.1 = (f32[256,1024]{1,0:T(8,128)}, f32[256,1024]{1,0:T(8,128)S(1)}, u32[]{:S(2)}) copy-start(f32[256,1024]{1,0:T(8,128)S(1)} %fusion.6) | copy-start | bytes 3145732
  48.2 0.6 copy-start.5
  52.5 0.7 copy-start.10
  52.5 1.9 %copy-start.2 = (f32[256,1024]{1,0:T(8,128)S(1)}, f32[256,1024]{1,0:T(8,128)}, u32[]{:S(2)}) copy-start(f32[256,1024]{1,0:T(8,128)} %copy-done.1) | copy-start | bytes 3145732
  52.5 1.9 %copy-start.4 = (bf16[2,1024,128]{2,1,0:T(8,128)(2,1)S(1)}, bf16[2,1024,128]{2,1,0:T(8,128)(2,1)}, u32[]{:S(2)}) copy-start(bf16[2,1024,128]{2,1,0:T(8,128)(2,1)} %copy-done.3) | copy-start | bytes 1572868
  52.5 1.9 %copy-start.6 = (bf16[128,2,128]{2,1,0:T(2,128)(2,1)S(1)}, bf16[128,2,128]{2,1,0:T(2,128)(2,1)}, u32[]{:S(2)}) copy-start(bf16[128,2,128]{2,1,0:T(2,128)(2,1)} %copy-done.5) | copy-start | bytes 196612
Sparse Core Ops, SparseCore 0:
  52.6 63.7 all-reduce.2
where the time goes:
time: 125 us
  waiting for transfers between devices  80.9 us (65%)
  between operations  14.8 us (12%)
  local copies, waits for them, and re-layouts  10.1 us (8%)
  blocking collectives  9.86 us (8%)
  starting transfers between devices  6.48 us (5%)
  matrix products  2.08 us (2%)
    unnamed x2, waiting for transfers between devices  60.9 us
    all_to_all x1, waiting for transfers between devices, body(): lax.all_to_all(out_weight, 'head', split_axis=1, concat_axis=0, tiled=True)  20 us
    all_gather x1, blocking collectives, body(): all_kv = lax.all_gather(own_kv, 'seq', axis=1, tiled=True)  9.86 us
    all_to_all x1, starting transfers between devices, body(): lax.all_to_all(out_weight, 'head', split_axis=1, concat_axis=0, tiled=True)  6.48 us
    unnamed x25, local copies, waits for them, and re-layouts  5.83 us
    dot_general x1, local copies, waits for them, and re-layouts, body(): jnp.einsum('td,thc->dhc', out_grad, attn, preferred_element_type=jnp.floa...  3.14 us
  transfers between devices with their start and end apart: 2, of which 2 were waited for; matrix products, arithmetic and copies ran while one was open for 2% of the time, Pallas kernels for 0%

commit v1 on v0

--- a/solution.py
+++ b/solution.py
@@ -56,7 +56,9 @@
     zeros_col = jnp.zeros((row_total, 1), jnp.float32)
     zeros_rows = jnp.zeros((row_total, HD), jnp.float32)
     lowest_col = jnp.full((row_total, 1), big_negative, jnp.float32)
-    all_kv = lax.all_gather(own_kv, "seq", axis=1, tiled=True)
+    all_kv = jnp.concatenate(
+        lax.all_to_all(jnp.stack([own_kv] * lax.axis_size("seq")), "seq", 0, 0), axis=1
+    )
 
     def run_sweep(step_fn, init):
         return sweep(step_fn, init, all_kv, 0, positions)

time: 125 us -> 136 us (1.088)
  waiting for transfers between devices: 80.9 us -> 97.4 us
  blocking collectives: 9.86 us -> 0 us
  starting transfers between devices: 6.48 us -> 10.1 us
    all_gather x1 -> x0, blocking collectives: 9.86 us -> none  [body(): all_kv = lax.all_gather(own_kv, 'seq', axis=1, tiled=True)]
    all_to_all x0 -> x1, waiting for transfers between devices: none -> 8.41 us  [body(): lax.all_to_all(jnp.stack([own_kv] * lax.axis_size('seq')), 'seq', 0, 0)]
    all_to_all x1, waiting for transfers between devices: 20 us -> 27.5 us  [body(): lax.all_to_all(out_weight, 'head', split_axis=1, concat_axis=0, tiled=True)]
    all_to_all x0 -> x1, starting transfers between devices: none -> 5.2 us  [body(): lax.all_to_all(jnp.stack([own_kv] * lax.axis_size('seq')), 'seq', 0, 0)]
    another operation x0 -> x1, local copies, waits for them, and re-layouts: none -> 1.88 us  [body(): jnp.stack([own_kv] * lax.axis_size('seq'))]
    all_to_all x1, starting transfers between devices: 6.48 us -> 4.87 us  [body(): lax.all_to_all(out_weight, 'head', split_axis=1, concat_axis=0, tiled=True)]
  transfers between devices with their start and end apart: 2 -> 3, of which waited for: 2 -> 3; matrix products, arithmetic and copies ran while one was open for 2% -> 3% of each run, Pallas kernels for 0% -> 0%
where the time goes in v1:
time: 136 us
  waiting for transfers between devices  97.4 us (72%)
  between operations  14.8 us (11%)
  local copies, waits for them, and re-layouts  10.7 us (8%)
  starting transfers between devices  10.1 us (7%)
  matrix products  2.08 us (2%)
    unnamed x2, waiting for transfers between devices  61.5 us
    all_to_all x1, waiting for transfers between devices, body(): lax.all_to_all(out_weight, 'head', split_axis=1, concat_axis=0, tiled=True)  27.5 us
    all_to_all x1, waiting for transfers between devices, body(): lax.all_to_all(jnp.stack([own_kv] * lax.axis_size('seq')), 'seq', 0, 0)  8.41 us
    all_to_all x1, starting transfers between devices, body(): lax.all_to_all(jnp.stack([own_kv] * lax.axis_size('seq')), 'seq', 0, 0)  5.2 us
    all_to_all x1, starting transfers between devices, body(): lax.all_to_all(out_weight, 'head', split_axis=1, concat_axis=0, tiled=True)  4.87 us
    unnamed x25, local copies, waits for them, and re-layouts  4.52 us
    dot_general x1, local copies, waits for them, and re-layouts, body(): jnp.einsum('td,thc->dhc', out_grad, attn, preferred_element_type=jnp.floa...  3.11 us
  transfers between devices with their start and end apart: 3, of which 3 were waited for; matrix products, arithmetic and copies ran while one was open for 3% of the time, Pallas kernels for 0%

profile of v1, /device:TPU:0, one launch (start us, length us, event | category | flops | bytes accessed | tf_op | source)
XLA Modules:
  0.0 135.8 jit_solution(11906673634596615019)
XLA Ops:
  7.2 0.0 copy-start
  7.2 0.0 copy-start.3
  7.2 1.9 %stack.2 = bf16[8,2,128,128]{3,2,1,0:T(8,128)(2,1)} broadcast(bf16[2,128,128]{2,1,0:T(8,128)(2,1)} %param.6), dimensions={1,2,3} | broadcast | bytes 589824 | tf_op jit(solution)/shard_map/stack | solution.py:60
  9.1 5.2 %all-to-all-start = ((bf16[8,2,128,128]{3,2,1,0:T(8,128)(2,1)}), bf16[8,2,128,128]{3,2,1,0:T(8,128)(2,1)S(1)}, u32[]{:S(2)}, u32[]{:S(2)}) async-start(bf16[8,2,128,128]{3,2,1,0:T(8,128)(2,1)} %stack.2), calls=%async_computation | async-start | bytes 1048576 | tf_op jit(solution)/shard_map/all_to_all | solution.py:60
  14.3 0.0 copy-done.3
  14.3 1.3 copy.14
  15.6 0.0 copy-start.8
  15.6 0.0 copy-start.9
  15.6 8.4 %all-to-all-done = bf16[8,2,128,128]{3,2,1,0:T(8,128)(2,1)S(1)} async-done(((bf16[8,2,128,128]{3,2,1,0:T(8,128)(2,1)}), bf16[8,2,128,128]{3,2,1,0:T(8,128)(2,1)S(1)}, u32[]{:S(2)}, u32[]{:S(2)}) %all-to-all-start) | async-done | bytes 524320 | tf_op jit(solution)/shard_map/all_to_all | solution.py:60
  24.0 4.9 %all-to-all-start.1 = ((bf16[640,8,128]{2,0,1:T(8,128)(2,1)}), bf16[640,8,128]{2,0,1:T(8,128)(2,1)S(1)}, u32[]{:S(2)}, u32[]{:S(2)}) async-start(bf16[640,8,128]{2,0,1:T(8,128)(2,1)} %copy.14), calls=%async_computation.1 | async-start | bytes 2621440 | tf_op jit(solution)/shard_map/all_to_all | solution.py:51
  28.9 0.0 all-reduce.3.cloned.1.call-start
  28.9 0.0 copy-done.8
  28.9 0.0 copy-done.9
  28.9 0.1 dynamic_slice.16
  29.0 0.1 broadcast_in_dim.38
  29.1 0.1 le.51
  29.3 0.0 copy-start.4
  29.3 0.4 fusion.16
  29.7 0.4 fusion.7
  30.1 0.3 fusion.6
  30.4 0.0 copy-done.4
  30.4 0.0 copy-start.1
  30.4 27.5 %all-to-all-done.1 = bf16[640,8,128]{2,0,1:T(8,128)(2,1)S(1)} async-done(((bf16[640,8,128]{2,0,1:T(8,128)(2,1)}), bf16[640,8,128]{2,0,1:T(8,128)(2,1)S(1)}, u32[]{:S(2)}, u32[]{:S(2)}) %all-to-all-start.1) | async-done | bytes 1310752 | tf_op jit(solution)/shard_map/all_to_all | solution.py:51
  57.9 0.1 copy.15
  58.0 0.0 copy-done
  58.1 0.4 convolution_convert_fusion
  58.4 0.1 copy.16
  58.5 0.0 copy-start.6
  58.5 0.0 copy-done.1
  58.5 0.4 fusion.15
  58.9 0.2 copy-done.6
  59.1 0.5 convolution_bitcast_fusion
  59.7 3.1 %copy.18 = f32[2560,2,128]{2,1,0:T(2,128)} copy(f32[2560,2,128]{0,2,1:T(8,128)S(1)} %convolution_bitcast_fusion) | data formatting | bytes 5242880 | tf_op jit(solution)/shard_map/td,thc->dhc/dot_general | solution.py:101
  62.8 0.0 copy-start.10
  62.8 0.0 copy-start.2
  62.8 0.0 copy-start.5
  62.8 0.0 copy-start.7
  62.8 0.0 all-reduce.3.cloned.1.call-update
  62.8 0.6 copy-done.10
  63.4 0.6 dynamic-slice
  64.7 0.0 copy-done.2
  64.7 0.0 copy-done.5
  64.7 0.0 copy-done.7
  64.7 0.4 fusion.5
  65.1 0.7 reshape.48
  65.8 61.5 %all-reduce.3.cloned.1.call-done = f32[2560,2,128]{2,1,0:T(2,128)} async-done(((f32[2560,2,128]{2,1,0:T(2,128)}), f32[2560,2,128]{2,1,0:T(2,128)}) %all-reduce.3.cloned.1.call-update) | async-done | bytes 2621456
  127.3 1.7 %constant_dynamic-slice_fusion = f32[320,2,128]{2,1,0:T(2,128)} fusion(f32[2560,2,128]{2,1,0:T(2,128)} %all-reduce.3.cloned.1.call-done, u32[]{:T(128)S(6)} %multiply.1), kind=kLoop, calls=%fused_computation.21 | loop fusion | bytes 655364
  (4 shorter events, 0.1 us)
Async XLA Ops:
  7.2 50.9 %copy-start = (bf16[128,2560]{1,0:T(8,128)(2,1)S(1)}, bf16[128,2560]{1,0:T(8,128)(2,1)}, u32[]{:S(2)}) copy-start(bf16[128,2560]{1,0:T(8,128)(2,1)} %param.8) | copy-start | bytes 1966084
  7.2 7.1 %copy-start.3 = (bf16[640,8,128]{2,1,0:T(8,128)(2,1)S(1)}, bf16[640,8,128]{2,1,0:T(8,128)(2,1)}, u32[]{:S(2)}) copy-start(bf16[640,8,128]{2,1,0:T(8,128)(2,1)} %param.7) | copy-start | bytes 3932164
  9.1 14.9 %all-to-all-start = ((bf16[8,2,128,128]{3,2,1,0:T(8,128)(2,1)}), bf16[8,2,128,128]{3,2,1,0:T(8,128)(2,1)S(1)}, u32[]{:S(2)}, u32[]{:S(2)}) async-start(bf16[8,2,128,128]{3,2,1,0:T(8,128)(2,1)} %stack.2), calls=%async_computation | async-start | bytes 1048576 | tf_op jit(solution)/shard_map/all_to_all | solution.py:60
  15.6 13.3 %copy-start.8 = (bf16[128,256]{1,0:T(8,128)(2,1)S(1)}, bf16[128,256]{1,0:T(8,128)(2,1)}, u32[]{:S(2)}) copy-start(bf16[128,256]{1,0:T(8,128)(2,1)} %param.5) | copy-start | bytes 196612
  15.6 13.3 %copy-start.9 = (s32[1024]{0:T(1024)S(1)}, s32[1024]{0:T(1024)}, u32[]{:S(2)}) copy-start(s32[1024]{0:T(1024)} %param.9) | copy-start | bytes 12292
  24.0 34.0 %all-to-all-start.1 = ((bf16[640,8,128]{2,0,1:T(8,128)(2,1)}), bf16[640,8,128]{2,0,1:T(8,128)(2,1)S(1)}, u32[]{:S(2)}, u32[]{:S(2)}) async-start(bf16[640,8,128]{2,0,1:T(8,128)(2,1)} %copy.14), calls=%async_computation.1 | async-start | bytes 2621440 | tf_op jit(solution)/shard_map/all_to_all | solution.py:51
  28.9 98.4 %all-reduce.3.cloned.1.call-start = ((), (), s32[]{:S(2)}) async-start(), calls=%async_computation.2 | async-start | bytes 5242880
  29.3 1.1 copy-start.4
  30.4 28.1 %copy-start.1 = (f32[256,1024]{1,0:T(8,128)}, f32[256,1024]{1,0:T(8,128)S(1)}, u32[]{:S(2)}) copy-start(f32[256,1024]{1,0:T(8,128)S(1)} %fusion.6) | copy-start | bytes 3145732
  58.5 0.6 copy-start.6
  62.8 0.7 copy-start.10
  62.8 1.9 %copy-start.2 = (f32[256,1024]{1,0:T(8,128)S(1)}, f32[256,1024]{1,0:T(8,128)}, u32[]{:S(2)}) copy-start(f32[256,1024]{1,0:T(8,128)} %copy-done.1) | copy-start | bytes 3145732
  62.8 1.9 %copy-start.5 = (bf16[1,8,128,128]{3,2,0,1:T(8,128)(2,1)S(1)}, bf16[1,8,128,128]{3,2,0,1:T(8,128)(2,1)}, u32[]{:S(2)}) copy-start(bf16[1,8,128,128]{3,2,0,1:T(8,128)(2,1)} %copy-done.4) | copy-start | bytes 786436
  62.8 1.9 %copy-start.7 = (bf16[128,2,128]{2,1,0:T(2,128)(2,1)S(1)}, bf16[128,2,128]{2,1,0:T(2,128)(2,1)}, u32[]{:S(2)}) copy-start(bf16[128,2,128]{2,1,0:T(2,128)(2,1)} %copy-done.6) | copy-start | bytes 196612
Sparse Core Ops, SparseCore 0:
  62.9 64.2 all-reduce.2
